TPU v7x, 256 devices: a whole 4x4x8 slice. The times are simulated.
256 devices in a mesh: rows: 32 (over y, x, core), cols: 8 (over z).
Axes of the slice: x: 4, y: 4, z: 8, core: 2. Of those that a mesh axis runs over, the one named last changes fastest.
Arguments:
- one_query: float32 [8192, 8192], P('rows', 'cols'), may hold values from -0.125 to 0.125
- other_query: float32 [8192, 8192], P('rows', 'cols'), may hold values from -0.0625 to 0.0625
- one_key: float32 [8192, 512], P('rows', 'cols'), may hold values from -0.125 to 0.125
- other_key: float32 [8192, 512], P('rows', 'cols'), may hold values from -0.0625 to 0.0625
- one_value: float32 [8192, 512], P('rows', 'cols'), may hold values from -0.125 to 0.125
- other_value: float32 [8192, 512], P('rows', 'cols'), may hold values from -0.0625 to 0.0625
- mix_share: float32 [8192], P('rows'), may hold values from 0.2 to 0.8
- norm_gain: float32 [8192], P('rows'), may hold values from 0.25 to 1.75
Outputs:
- serve_query: bfloat16 [8192, 8192], P(None, 'cols')
- serve_key: bfloat16 [8192, 512], P(None, 'cols')
- serve_value: bfloat16 [8192, 512], P(None, 'cols')
- scale_query: float32 [8192], P('cols')
- scale_key: float32 [512], P('cols')
- scale_value: float32 [512], P('cols')
All inputs are finite; a program needn't handle non-finite values. Where the computation divides by a largest or mean magnitude, that divisor is 1e-20 or more.
Results may differ from a plain program's by a relative error of at most 0.001.
Values may be sent and summed in bfloat16 or wider, within the bound.
A program may use at most 128 MiB of HBM per device.

v0:
```python
import jax
import jax.numpy as jnp
from jax import lax
from jax.sharding import PartitionSpec as P

D_MODEL = 8192


def from_everyone(x, axis):
    count = lax.axis_size(axis)
    return lax.all_to_all(jnp.broadcast_to(x[None], (count, *x.shape)), axis, 0, 0, tiled=True)


def taken_together(x, axis):
    everything = from_everyone(x, axis)
    return jnp.sum(everything, axis=0)


def together(arrays, axis):
    vector, at, finished = (jnp.concatenate([a.reshape(-1) for a in arrays]), 0, [])
    subtotal = taken_together(vector, axis)
    for a in arrays:
        finished.append(subtotal[at : at + a.size].reshape(a.shape))
        at += a.size
    return tuple(finished)


def in_one_piece(arrays, axis, dim, along):
    both = jnp.concatenate(arrays, axis=along)
    filled, at, finished = (lax.all_gather(both, axis, axis=dim, tiled=True), 0, [])
    for a in arrays:
        finished.append(lax.slice_in_dim(filled, at, at + a.shape[along], axis=along))
        at += a.shape[along]
    return tuple(finished)


def local(one_query, other_query, one_key, other_key, one_value, other_value, mix_share, norm_gain):
    fresh_query = mix_share[:, None] * one_query + (1.0 - mix_share[:, None]) * other_query
    fresh_key = mix_share[:, None] * one_key + (1.0 - mix_share[:, None]) * other_key
    fresh_value = mix_share[:, None] * one_value + (1.0 - mix_share[:, None]) * other_value
    fresh_gained_query = fresh_query * norm_gain[:, None]
    fresh_gained_key = fresh_key * norm_gain[:, None]
    fresh_gained_value = fresh_value * norm_gain[:, None]
    total_query, total_key, total_value = together(
        (
            jnp.sum(jnp.abs(fresh_gained_query), axis=0),
            jnp.sum(jnp.abs(fresh_gained_key), axis=0),
            jnp.sum(jnp.abs(fresh_gained_value), axis=0),
        ),
        "rows",
    )
    scale_query = total_query / D_MODEL
    scale_key = total_key / D_MODEL
    scale_value = total_value / D_MODEL
    narrow_query, narrow_key, narrow_value = (
        (fresh_gained_query / scale_query).astype(jnp.bfloat16),
        (fresh_gained_key / scale_key).astype(jnp.bfloat16),
        (fresh_gained_value / scale_value).astype(jnp.bfloat16),
    )
    serve_query, serve_key, serve_value = in_one_piece(
        (narrow_query, narrow_key, narrow_value), "rows", 0, 1
    )
    return (serve_query, serve_key, serve_value, scale_query, scale_key, scale_value)


def solution(mesh):
    return jax.shard_map(
        local,
        mesh=mesh,
        in_specs=(
            P("rows", "cols"),
            P("rows", "cols"),
            P("rows", "cols"),
            P("rows", "cols"),
            P("rows", "cols"),
            P("rows", "cols"),
            P("rows"),
            P("rows"),
        ),
        out_specs=(
            P(None, "cols"),
            P(None, "cols"),
            P(None, "cols"),
            P("cols"),
            P("cols"),
            P("cols"),
        ),
        check_vma=False,
    )
```

profile of v0, /device:TPU:1, one launch (start us, length us, event | category | flops | bytes accessed | tf_op | source)
XLA Modules:
  0.0 165.5 jit_solution(11187049639530629452)
XLA Ops:
  7.2 0.0 copy-start
  7.2 0.0 all-gather.2.cloned.1.call-start
  7.2 0.8 broadcast_subtract_fusion
  8.0 1.6 copy.20
  9.5 0.0 copy-done
  9.6 0.0 copy-start.5
  9.6 0.0 copy-start.7
  9.6 0.3 copy.21
  9.9 0.3 copy-done.5
  10.2 0.0 copy-done.7
  10.3 0.3 abs_reduce_fusion
  10.5 0.5 copy-done.1
  11.1 0.0 copy-done.2
  11.1 0.0 copy-done.3
  11.2 0.0 copy-done.4
  11.2 0.1 abs_reduce_fusion.1
  11.3 0.1 concatenate.6
  11.4 0.1 broadcast_in_dim.2
  11.5 16.1 %all_to_all.6 = f32[32,1,1152]{2,1,0:T(1,128)S(1)} all-to-all(f32[32,1,1152]{2,1,0:T(1,128)S(1)} %broadcast_in_dim.2), channel_id=1, replica_groups=mesh['rows'=32,'cols'=8] {'rows'}, dimensions={0} | all-to-all | bytes 294912 | tf_op jit(solution)/shard_map/all_to_all | solution.py:11
  27.6 0.1 reduce_sum.39
  27.7 0.1 slice_multiply_fusion.2
  27.8 0.2 divide_convert_fusion
  28.0 0.4 copy-done.6
  28.4 0.0 copy-done.8
  28.4 0.0 copy-done.9
  28.4 0.1 divide_convert_fusion.2
  28.5 0.9 pad_maximum_fusion
  29.4 0.0 all-gather.2.cloned.1.call-update
  29.4 90.0 %all-gather.2.cloned.1.call-done = bf16[8192,1152]{0,1:T(8,128)(2,1)} async-done(((bf16[256,1152]{0,1:T(8,128)(2,1)}), bf16[8192,1152]{0,1:T(8,128)(2,1)}) %all-gather.2.cloned.1.call-update) | async-done | bytes 18874384 | tf_op jit(solution)/shard_map/all_gather | solution.py:30
  119.4 13.9 %slice.27 = bf16[8192,1024]{0,1:T(8,128)(2,1)} slice(bf16[8192,1152]{0,1:T(8,128)(2,1)} %all-gather.2.cloned.1.call-done), slice={[0:8192], [0:1024]} | slice | bytes 33554432 | tf_op jit(solution)/shard_map/slice | solution.py:32
  133.3 22.4 %copy.23 = bf16[8192,1024]{1,0:T(8,128)(2,1)} copy(bf16[8192,1024]{0,1:T(8,128)(2,1)} %slice.27) | data formatting | bytes 33554432
  155.7 3.0 %fusion = (bf16[8192,64]{0,1:T(8,128)(2,1)}, bf16[8192,64]{0,1:T(8,128)(2,1)}) fusion(bf16[8192,1152]{0,1:T(8,128)(2,1)} %all-gather.2.cloned.1.call-done), kind=kLoop, calls=%fused_computation.14 | loop fusion | bytes 4194304 | tf_op jit(solution)/shard_map/slice | solution.py:32
  (8 shorter events, 0.0 us)
Async XLA Ops:
  7.2 2.4 %copy-start = (f32[256,1024]{1,0:T(8,128)S(1)}, f32[256,1024]{1,0:T(8,128)}, u32[]{:S(2)}) copy-start(f32[256,1024]{1,0:T(8,128)} %param.9) | copy-start | bytes 3145732
  7.2 112.2 %all-gather.2.cloned.1.call-start = ((), (), s32[]{:S(2)}) async-start(), calls=%async_computation.1 | async-start | bytes 19464192 | tf_op jit(solution)/shard_map/all_gather | solution.py:30
  9.6 0.7 copy-start.5
  9.6 0.7 copy-start.7
  10.3 0.8 copy-start.1
  10.3 0.9 copy-start.2
  10.3 0.9 copy-start.3
  10.3 0.9 copy-start.4
  27.8 0.6 copy-start.8
  27.8 0.6 copy-start.9
  27.8 0.6 copy-start.6
Sparse Core Ops, SparseCore 0:
  29.5 89.8 all-gather.1
where the time goes:
time: 166 us
  waiting for transfers between devices  90 us (54%)
  local copies, waits for them, and re-layouts  42.7 us (26%)
  blocking collectives  16.1 us (10%)
  between operations  14.1 us (8%)
  other arithmetic  2.52 us (2%)
    all_gather x1, waiting for transfers between devices, in_one_piece(): lax.all_gather(both, axis, axis=dim, tiled=True)  90 us
    unnamed x23, local copies, waits for them, and re-layouts  25.6 us
    slice x2, local copies, waits for them, and re-layouts, in_one_piece(): lax.slice_in_dim(filled, at, at + a.shape[along], axis=along)  16.9 us
    all_to_all x1, blocking collectives, from_everyone(): lax.all_to_all(jnp.broadcast_to(x[None], (count, *x.shape)), axis, 0, 0,...  16.1 us
  transfers between devices with their start and end apart: 1, of which 1 were waited for; matrix products, arithmetic and copies ran while one was open for 0% of the time, Pallas kernels for 0%

commit v1 on v0

v1 whole, which is shorter than its diff:
```python
import functools

import jax
import jax.numpy as jnp
from jax import lax
from jax.experimental import pallas as pl
from jax.experimental.pallas import tpu as pltpu
from jax.sharding import PartitionSpec as P

D_MODEL = 8192
MESH = pl.DeviceIdType.MESH
NX, NY, NC = 4, 4, 2
UNIT = 64

PLUS_X = (
    (0, 0, 0), (0, 0, 1), (0, 0, 2), (-1, 0, 0), (0, 0, 3), (0, -1, 2), (0, 1, 2), (-1, 0, 2),
    (0, 2, 2), (-1, -1, 2), (0, -1, 3), (-1, 1, 2), (0, 1, 3), (-1, 2, 2), (0, 2, 3),
)


def mirrored(items):
    return tuple((-dx, -dy, q ^ 1) for dx, dy, q in items)


def turned(items):
    return tuple((dy, dx, q ^ 2) for dx, dy, q in items)


LINKS = (
    (1, 0, PLUS_X),
    (-1, 0, mirrored(PLUS_X)),
    (0, 1, turned(PLUS_X)),
    (0, -1, mirrored(turned(PLUS_X))),
)


def received(link, slot):
    sx, sy, items = LINKS[link]
    dx, dy, q = items[slot]
    return ((dx - sx) % NX, (dy - sy) % NY, q)


STEPS = len(PLUS_X)
ARRIVAL = {received(link, slot): slot for link in range(4) for slot in range(STEPS)}


def due(link, slot):
    dx, dy, q = LINKS[link][2][slot]
    return -1 if (dx, dy) == (0, 0) else ARRIVAL[(dx % NX, dy % NY, q)]


def gather_kernel(
    one_q, other_q, one_k, other_k, one_v, other_v, mix, gain,
    full, total,
    in_one_q, in_other_q, in_one_kv, in_other_kv, in_mix, in_gain,
    gained, part, row_sums, mid, col_sums,
    load_sem, row_send, row_recv, col_send, col_recv, send_sem, recv_sem, pair_recv,
):
    me = lax.axis_index("rows")
    core = lax.rem(me, NC)
    chip = lax.div(me, NC)
    x = lax.rem(chip, NX)
    y = lax.div(chip, NX)

    def at(dx, dy):
        return lax.rem(y + dy % NY, NY) * NX + lax.rem(x + dx % NX, NX)

    def device(dx, dy, c):
        return {"rows": at(dx, dy) * NC + c}

    row_peers = [(1, 0, core), (3, 0, core), (2, 0, core), (1, 0, 1 - core), (3, 0, 1 - core), (2, 0, 1 - core), (0, 0, 1 - core)]
    col_peers = [(0, 1, core), (0, 3, core), (0, 2, core)]
    barrier = pltpu.get_barrier_semaphore()
    for peer in row_peers + col_peers:
        pl.semaphore_signal(barrier, inc=1, device_id=device(*peer), device_id_type=MESH)

    loads = [
        pltpu.make_async_copy(mix, in_mix, load_sem.at[0]),
        pltpu.make_async_copy(gain, in_gain, load_sem.at[1]),
        pltpu.make_async_copy(one_k, in_one_kv.at[pl.ds(0, 64)], load_sem.at[2]),
        pltpu.make_async_copy(one_v, in_one_kv.at[pl.ds(64, 64)], load_sem.at[3]),
        pltpu.make_async_copy(other_k, in_other_kv.at[pl.ds(0, 64)], load_sem.at[4]),
        pltpu.make_async_copy(other_v, in_other_kv.at[pl.ds(64, 64)], load_sem.at[5]),
    ]
    halves = []
    for h in range(2):
        rows = pl.ds(128 * h, 128)
        halves.append([
            pltpu.make_async_copy(one_q.at[rows], in_one_q.at[rows], load_sem.at[6 + 2 * h]),
            pltpu.make_async_copy(other_q.at[rows], in_other_q.at[rows], load_sem.at[7 + 2 * h]),
        ])
    for copy in loads + halves[0] + halves[1]:
        copy.start()
    for copy in loads:
        copy.wait()

    m, g = in_mix[...], in_gain[...]
    kv = (m * in_one_kv[...] + (1.0 - m) * in_other_kv[...]) * g
    kv_sum = jnp.sum(jnp.abs(kv), axis=1, keepdims=True)
    gained[pl.ds(0, 128), pl.ds(1024, 128)] = kv[:, :128]
    gained[pl.ds(128, 128), pl.ds(1024, 128)] = kv[:, 128:]
    part[:, pl.ds(1024, 128)] = jnp.transpose(jnp.broadcast_to(kv_sum, (128, 128)))[:1]

    sums = jnp.zeros((8, 1024), jnp.float32)
    for h in range(2):
        for copy in halves[h]:
            copy.wait()
        m_rows = jnp.transpose(jnp.broadcast_to(m[:, 128 * h : 128 * h + 128], (128, 128)))
        g_rows = jnp.transpose(jnp.broadcast_to(g[:, 128 * h : 128 * h + 128], (128, 128)))
        for t in range(16):
            rows = pl.ds(128 * h + 8 * t, 8)
            mt = jnp.concatenate([m_rows[8 * t : 8 * t + 8]] * 8, axis=1)
            gt = jnp.concatenate([g_rows[8 * t : 8 * t + 8]] * 8, axis=1)
            value = (mt * in_one_q[rows, :] + (1.0 - mt) * in_other_q[rows, :]) * gt
            gained[rows, pl.ds(0, 1024)] = value
            sums = sums + jnp.abs(value)
    part[:, pl.ds(0, 1024)] = jnp.sum(sums, axis=0, keepdims=True)

    pl.semaphore_wait(barrier, len(row_peers) + len(col_peers))
    own = x * NC + core
    copies = []
    for i, (dx, dy, c) in enumerate(row_peers):
        copies.append(pltpu.make_async_remote_copy(
            src_ref=part, dst_ref=row_sums.at[own], send_sem=row_send.at[i],
            recv_sem=row_recv.at[i], device_id=device(dx, dy, c), device_id_type=MESH,
        ))
        copies[-1].start()
    row_sums[own] = part[...]
    for copy in copies:
        copy.wait()
    subtotal = row_sums[0]
    for i in range(1, NX * NC):
        subtotal = subtotal + row_sums[i]
    mid[...] = subtotal
    copies = []
    for i, (dx, dy, c) in enumerate(col_peers):
        copies.append(pltpu.make_async_remote_copy(
            src_ref=mid, dst_ref=col_sums.at[y], send_sem=col_send.at[i],
            recv_sem=col_recv.at[i], device_id=device(dx, dy, c), device_id_type=MESH,
        ))
        copies[-1].start()
    col_sums[y] = mid[...]
    for copy in copies:
        copy.wait()
    subtotal = col_sums[0]
    for i in range(1, NY):
        subtotal = subtotal + col_sums[i]
    scale = subtotal / D_MODEL
    total[...] = scale
    inverse = 1.0 / scale
    inverse_kv = jnp.transpose(jnp.broadcast_to(inverse[:, 1024:], (128, 128)))

    def rows_of(dx, dy, q):
        return pl.ds(pl.multiple_of((core * NX * NY + at(dx, dy)) * 256 + q * UNIT, UNIT), UNIT)

    def send(link, slot):
        sx, sy, items = LINKS[link]
        rows = rows_of(*items[slot])
        pltpu.make_async_remote_copy(
            src_ref=full.at[rows], dst_ref=full.at[rows], send_sem=send_sem,
            recv_sem=recv_sem.at[link, slot], device_id=device(sx, sy, core), device_id_type=MESH,
        ).start()

    def share(dx, dy, q):
        rows = rows_of(dx, dy, q)
        pltpu.make_async_remote_copy(
            src_ref=full.at[rows], dst_ref=full.at[rows], send_sem=send_sem,
            recv_sem=pair_recv, device_id=device(0, 0, 1 - core), device_id_type=MESH,
        ).start()

    for q in range(4):
        rows = pl.ds(q * UNIT, UNIT)
        dst = rows_of(0, 0, q)
        full[dst, pl.ds(0, 1024)] = (gained[rows, pl.ds(0, 1024)] * inverse[:, :1024]).astype(jnp.bfloat16)
        half = (q % 2) * UNIT
        full[dst, pl.ds(1024, 128)] = (gained[rows, pl.ds(1024, 128)] * inverse_kv[half : half + UNIT]).astype(jnp.bfloat16)

    sent = [0, 0, 0, 0]
    for slot in range(-1, STEPS):
        if slot >= 0:
            for link in range(4):
                dx, dy, q = received(link, slot)
                rows = rows_of(dx, dy, q)
                pltpu.make_async_remote_copy(
                    src_ref=full.at[rows], dst_ref=full.at[rows], send_sem=send_sem,
                    recv_sem=recv_sem.at[link, slot], device_id=device(0, 0, 1 - core), device_id_type=MESH,
                ).wait_recv()
                share(dx, dy, q)
        for link in range(4):
            while sent[link] < STEPS and due(link, sent[link]) <= slot:
                send(link, sent[link])
                sent[link] += 1
        if slot == -1:
            for q in range(4):
                share(0, 0, q)

    other = pl.ds(pl.multiple_of((1 - core) * 4096, 4096), 4096)
    pltpu.make_async_copy(full.at[other], full.at[other], pair_recv).wait()
    everything = pl.ds(0, (4 * STEPS + 64) * UNIT)
    pltpu.make_async_copy(full.at[everything], full.at[everything], send_sem).wait()


def write_kernel(full, total, query, key, value, scale_q, scale_k, scale_v, sem):
    copies = [
        pltpu.make_async_copy(total.at[:, pl.ds(0, 1024)], scale_q, sem.at[0]),
    ]
    n = 1
    for c in range(NC):
        for p in range(NX * NY):
            src, dst = (c * NX * NY + p) * 256, (p * NC + c) * 256
            copies.append(pltpu.make_async_copy(full.at[pl.ds(src, 256), pl.ds(0, 1024)], query.at[pl.ds(dst, 256)], sem.at[n]))
            n += 1
            for q in range(4):
                out = (key, value)[q % 2]
                copies.append(pltpu.make_async_copy(
                    full.at[pl.ds(src + q * UNIT, UNIT), pl.ds(1024, 128)],
                    out.at[:, pl.ds(dst + 128 * (q // 2), 128)],
                    sem.at[n],
                ))
                n += 1
    for copy in copies:
        copy.start()
    scale_k[...] = total[:, 1024:1088]
    scale_v[...] = total[:, 1088:1152]
    for copy in copies:
        copy.wait()


def local(one_query, other_query, one_key, other_key, one_value, other_value, mix_share, norm_gain):
    hbm = pl.BlockSpec(memory_space=pltpu.HBM)
    vmem = pl.BlockSpec(memory_space=pltpu.VMEM)
    f32, bf16 = jnp.float32, jnp.bfloat16
    full, total = pl.pallas_call(
        gather_kernel,
        out_shape=(pltpu.VMEM((8192, 1152), bf16), pltpu.VMEM((1, 1152), f32)),
        in_specs=[hbm] * 8,
        out_specs=(vmem, vmem),
        scratch_shapes=[
            pltpu.VMEM((256, 1024), f32),
            pltpu.VMEM((256, 1024), f32),
            pltpu.VMEM((128, 256), f32),
            pltpu.VMEM((128, 256), f32),
            pltpu.VMEM((1, 256), f32),
            pltpu.VMEM((1, 256), f32),
            pltpu.VMEM((256, 1152), f32),
            pltpu.VMEM((1, 1152), f32),
            pltpu.VMEM((8, 1, 1152), f32),
            pltpu.VMEM((1, 1152), f32),
            pltpu.VMEM((4, 1, 1152), f32),
            pltpu.SemaphoreType.DMA((10,)),
            pltpu.SemaphoreType.DMA((7,)),
            pltpu.SemaphoreType.DMA((7,)),
            pltpu.SemaphoreType.DMA((3,)),
            pltpu.SemaphoreType.DMA((3,)),
            pltpu.SemaphoreType.DMA,
            pltpu.SemaphoreType.DMA((4, STEPS)),
            pltpu.SemaphoreType.DMA,
        ],
        compiler_params=pltpu.CompilerParams(
            collective_id=0, has_side_effects=True, vmem_limit_bytes=16 * 2**20
        ),
        name="gather",
    )(*(
        pltpu.with_memory_space_constraint(a, pltpu.HBM)
        for a in (
            one_query, other_query, one_key.T, other_key.T, one_value.T, other_value.T,
            mix_share.reshape(1, 256), norm_gain.reshape(1, 256),
        )
    ))
    query, key, value, scale_q, scale_k, scale_v = pl.pallas_call(
        write_kernel,
        out_shape=(
            jax.ShapeDtypeStruct((8192, 1024), bf16),
            jax.ShapeDtypeStruct((64, 8192), bf16),
            jax.ShapeDtypeStruct((64, 8192), bf16),
            jax.ShapeDtypeStruct((1, 1024), f32),
            jax.ShapeDtypeStruct((1, 64), f32),
            jax.ShapeDtypeStruct((1, 64), f32),
        ),
        in_specs=[vmem, vmem],
        out_specs=[hbm] * 4 + [vmem] * 2,
        scratch_shapes=[pltpu.SemaphoreType.DMA((1 + 5 * 32,))],
        compiler_params=pltpu.CompilerParams(vmem_limit_bytes=4 * 2**20),
        name="write",
    )(full, total)
    return (query, key.T, value.T, scale_q.reshape(1024), scale_k.reshape(64), scale_v.reshape(64))


def solution(mesh):
    return jax.shard_map(
        local,
        mesh=mesh,
        in_specs=(
            P("rows", "cols"),
            P("rows", "cols"),
            P("rows", "cols"),
            P("rows", "cols"),
            P("rows", "cols"),
            P("rows", "cols"),
            P("rows"),
            P("rows"),
        ),
        out_specs=(
            P(None, "cols"),
            P(None, "cols"),
            P(None, "cols"),
            P("cols"),
            P("cols"),
            P("cols"),
        ),
        check_vma=False,
    )
```

time: 166 us -> 73.6 us (0.44)
  waiting for transfers between devices: 90 us -> 0 us
  Pallas kernels: 0 us -> 72.8 us
  local copies, waits for them, and re-layouts: 42.7 us -> 0 us
  blocking collectives: 16.1 us -> 0 us
  between operations: 14.1 us -> 0.64 us
  other arithmetic: 2.52 us -> 0 us
    all_gather x1 -> x0, waiting for transfers between devices: 90 us -> none  [in_one_piece(): lax.all_gather(both, axis, axis=dim, tiled=True)]
    pallas_call x0 -> x2, Pallas kernels: none -> 72.8 us  [the longest x1 64.4 us: local(): pl.pallas_call(gather_kernel, out_shape=(pltpu.VMEM((8192, 1152), bf16),...]
    unnamed x23 -> x0, local copies, waits for them, and re-layouts: 25.6 us -> none
    slice x2 -> x0, local copies, waits for them, and re-layouts: 16.9 us -> none  [in_one_piece(): lax.slice_in_dim(filled, at, at + a.shape[along], axis=along)]
    all_to_all x1 -> x0, blocking collectives: 16.1 us -> none  [from_everyone(): lax.all_to_all(jnp.broadcast_to(x[None], (count, *x.shape)), axis, 0, 0,...]
  transfers between devices with their start and end apart: 1 -> 0, of which waited for: 1 -> 0; matrix products, arithmetic and copies ran while one was open for 0% -> 0% of each run, Pallas kernels for 0% -> 0%
where the time goes in v1:
time: 73.6 us; the launch traced here: 73.4 us
  Pallas kernels  72.8 us (99%)
    pallas_call x1, Pallas kernels, local(): pl.pallas_call(gather_kernel, out_shape=(pltpu.VMEM((8192, 1152), bf16),...  64.4 us
    pallas_call x1, Pallas kernels, local(): pl.pallas_call(write_kernel, out_shape=(jax.ShapeDtypeStruct((8192, 1024)...  8.36 us

profile of v1, /device:TPU:1, one launch (start us, length us, event | category | flops | bytes accessed | tf_op | source)
XLA Modules:
  0.0 73.4 jit_solution(4463233225048142005)
XLA Ops:
  0.6 64.4 %gather.1 = (bf16[8192,1152]{1,0:T(8,128)(2,1)S(1)}, f32[1,1152]{1,0:T(1,128)S(1)}) custom-call(f32[256,1024]{1,0:T(8,128)} %one_q.1, f32[256,1024]{1,0:T(8,128)} %other_q.1, f32[64,256]{1,0:T(8,128)} %bitcast.11, f32[64,256]{1,0:T(8,128)} %bitcast.12, f32[64,256]{1,0:T(8,128)} %bitcast.13, f32[64,256]{1,0:T(8,128)} %bitcast.14, f32[1,256]{1,0:T(1,128)} %bitcast.15, ...), custom_call_target="tpu_custom_call" | custom-call | tf_op jit(solution)/shard_map/gather/pallas_call | solution.py:233
  65.1 8.4 %write.1 = (bf16[8192,1024]{1,0:T(8,128)(2,1)}, bf16[64,8192]{1,0:T(8,128)(2,1)}, bf16[64,8192]{1,0:T(8,128)(2,1)}, f32[1,1024]{1,0:T(1,128)}, f32[1,64]{1,0:T(1,128)}, /*index=5*/f32[1,64]{1,0:T(1,128)}) custom-call(bf16[8192,1152]{1,0:T(8,128)(2,1)S(1)} %get-tuple-element.14.full, f32[1,1152]{1,0:T(1,128)S(1)} %get-tuple-element.15.total), custom_call_target="tpu_custom_call" | custom-call | tf_op jit(solution)/shard_map/write/pallas_call | solution.py:270

commit v2 on v1

--- a/solution.py
+++ b/solution.py
@@ -52,9 +52,9 @@
 def gather_kernel(
     one_q, other_q, one_k, other_k, one_v, other_v, mix, gain,
     full, total,
-    in_one_q, in_other_q, in_one_kv, in_other_kv, in_mix, in_gain,
+    in_q, in_kv, in_vec,
     gained, part, row_sums, mid, col_sums,
-    load_sem, row_send, row_recv, col_send, col_recv, send_sem, recv_sem, pair_recv,
+    load_sem, sum_send, sum_recv, send_sem, recv_sem, pair_recv,
 ):
     me = lax.axis_index("rows")
     core = lax.rem(me, NC)
@@ -74,28 +74,28 @@
     for peer in row_peers + col_peers:
         pl.semaphore_signal(barrier, inc=1, device_id=device(*peer), device_id_type=MESH)
 
-    loads = [
-        pltpu.make_async_copy(mix, in_mix, load_sem.at[0]),
-        pltpu.make_async_copy(gain, in_gain, load_sem.at[1]),
-        pltpu.make_async_copy(one_k, in_one_kv.at[pl.ds(0, 64)], load_sem.at[2]),
-        pltpu.make_async_copy(one_v, in_one_kv.at[pl.ds(64, 64)], load_sem.at[3]),
-        pltpu.make_async_copy(other_k, in_other_kv.at[pl.ds(0, 64)], load_sem.at[4]),
-        pltpu.make_async_copy(other_v, in_other_kv.at[pl.ds(64, 64)], load_sem.at[5]),
+    small = [
+        pltpu.make_async_copy(mix, in_vec.at[0], load_sem.at[0]),
+        pltpu.make_async_copy(gain, in_vec.at[1], load_sem.at[0]),
     ]
-    halves = []
+    thin = [
+        pltpu.make_async_copy(one_k, in_kv.at[0, pl.ds(0, 64)], load_sem.at[1]),
+        pltpu.make_async_copy(one_v, in_kv.at[0, pl.ds(64, 64)], load_sem.at[1]),
+        pltpu.make_async_copy(other_k, in_kv.at[1, pl.ds(0, 64)], load_sem.at[1]),
+        pltpu.make_async_copy(other_v, in_kv.at[1, pl.ds(64, 64)], load_sem.at[1]),
+    ]
+    wide = []
     for h in range(2):
         rows = pl.ds(128 * h, 128)
-        halves.append([
-            pltpu.make_async_copy(one_q.at[rows], in_one_q.at[rows], load_sem.at[6 + 2 * h]),
-            pltpu.make_async_copy(other_q.at[rows], in_other_q.at[rows], load_sem.at[7 + 2 * h]),
-        ])
-    for copy in loads + halves[0] + halves[1]:
+        wide.append(pltpu.make_async_copy(one_q.at[rows], in_q.at[0, rows], load_sem.at[2 + h]))
+        wide.append(pltpu.make_async_copy(other_q.at[rows], in_q.at[1, rows], load_sem.at[2 + h]))
+    for copy in small + thin + wide:
         copy.start()
-    for copy in loads:
-        copy.wait()
-
-    m, g = in_mix[...], in_gain[...]
-    kv = (m * in_one_kv[...] + (1.0 - m) * in_other_kv[...]) * g
+    pltpu.make_async_copy(in_vec, in_vec, load_sem.at[0]).wait()
+    pltpu.make_async_copy(in_kv, in_kv, load_sem.at[1]).wait()
+
+    m, g = in_vec[0], in_vec[1]
+    kv = (m * in_kv[0] + (1.0 - m) * in_kv[1]) * g
     kv_sum = jnp.sum(jnp.abs(kv), axis=1, keepdims=True)
     gained[pl.ds(0, 128), pl.ds(1024, 128)] = kv[:, :128]
     gained[pl.ds(128, 128), pl.ds(1024, 128)] = kv[:, 128:]
@@ -103,45 +103,41 @@
 
     sums = jnp.zeros((8, 1024), jnp.float32)
     for h in range(2):
-        for copy in halves[h]:
-            copy.wait()
+        half = in_q.at[:, pl.ds(128 * h, 128)]
+        pltpu.make_async_copy(half, half, load_sem.at[2 + h]).wait()
         m_rows = jnp.transpose(jnp.broadcast_to(m[:, 128 * h : 128 * h + 128], (128, 128)))
         g_rows = jnp.transpose(jnp.broadcast_to(g[:, 128 * h : 128 * h + 128], (128, 128)))
         for t in range(16):
             rows = pl.ds(128 * h + 8 * t, 8)
             mt = jnp.concatenate([m_rows[8 * t : 8 * t + 8]] * 8, axis=1)
             gt = jnp.concatenate([g_rows[8 * t : 8 * t + 8]] * 8, axis=1)
-            value = (mt * in_one_q[rows, :] + (1.0 - mt) * in_other_q[rows, :]) * gt
+            value = (mt * in_q[0, rows, :] + (1.0 - mt) * in_q[1, rows, :]) * gt
             gained[rows, pl.ds(0, 1024)] = value
             sums = sums + jnp.abs(value)
     part[:, pl.ds(0, 1024)] = jnp.sum(sums, axis=0, keepdims=True)
 
     pl.semaphore_wait(barrier, len(row_peers) + len(col_peers))
     own = x * NC + core
-    copies = []
-    for i, (dx, dy, c) in enumerate(row_peers):
-        copies.append(pltpu.make_async_remote_copy(
-            src_ref=part, dst_ref=row_sums.at[own], send_sem=row_send.at[i],
-            recv_sem=row_recv.at[i], device_id=device(dx, dy, c), device_id_type=MESH,
-        ))
-        copies[-1].start()
+    for dx, dy, c in row_peers:
+        pltpu.make_async_remote_copy(
+            src_ref=part, dst_ref=row_sums.at[own], send_sem=sum_send.at[0],
+            recv_sem=sum_recv.at[0], device_id=device(dx, dy, c), device_id_type=MESH,
+        ).start()
     row_sums[own] = part[...]
-    for copy in copies:
-        copy.wait()
+    others = row_sums.at[pl.ds(0, len(row_peers))]
+    pltpu.make_async_copy(others, others, sum_recv.at[0]).wait()
     subtotal = row_sums[0]
     for i in range(1, NX * NC):
         subtotal = subtotal + row_sums[i]
     mid[...] = subtotal
-    copies = []
-    for i, (dx, dy, c) in enumerate(col_peers):
-        copies.append(pltpu.make_async_remote_copy(
-            src_ref=mid, dst_ref=col_sums.at[y], send_sem=col_send.at[i],
-            recv_sem=col_recv.at[i], device_id=device(dx, dy, c), device_id_type=MESH,
-        ))
-        copies[-1].start()
+    for dx, dy, c in col_peers:
+        pltpu.make_async_remote_copy(
+            src_ref=mid, dst_ref=col_sums.at[y], send_sem=sum_send.at[1],
+            recv_sem=sum_recv.at[1], device_id=device(dx, dy, c), device_id_type=MESH,
+        ).start()
     col_sums[y] = mid[...]
-    for copy in copies:
-        copy.wait()
+    others = col_sums.at[pl.ds(0, len(col_peers))]
+    pltpu.make_async_copy(others, others, sum_recv.at[1]).wait()
     subtotal = col_sums[0]
     for i in range(1, NY):
         subtotal = subtotal + col_sums[i]
@@ -198,32 +194,35 @@
     pltpu.make_async_copy(full.at[other], full.at[other], pair_recv).wait()
     everything = pl.ds(0, (4 * STEPS + 64) * UNIT)
     pltpu.make_async_copy(full.at[everything], full.at[everything], send_sem).wait()
-
-
-def write_kernel(full, total, query, key, value, scale_q, scale_k, scale_v, sem):
-    copies = [
-        pltpu.make_async_copy(total.at[:, pl.ds(0, 1024)], scale_q, sem.at[0]),
-    ]
-    n = 1
+    sums_sent = row_sums.at[pl.ds(0, len(row_peers))]
+    pltpu.make_async_copy(sums_sent, sums_sent, sum_send.at[0]).wait()
+    sums_sent = col_sums.at[pl.ds(0, len(col_peers))]
+    pltpu.make_async_copy(sums_sent, sums_sent, sum_send.at[1]).wait()
+
+
+def write_kernel(full, total, query, key, value, scale_q, scale_k, scale_v, near_k, near_v, sem):
+    copies = [pltpu.make_async_copy(total.at[:, pl.ds(0, 1024)], scale_q, sem.at[1])]
     for c in range(NC):
         for p in range(NX * NY):
             src, dst = (c * NX * NY + p) * 256, (p * NC + c) * 256
-            copies.append(pltpu.make_async_copy(full.at[pl.ds(src, 256), pl.ds(0, 1024)], query.at[pl.ds(dst, 256)], sem.at[n]))
-            n += 1
+            copies.append(pltpu.make_async_copy(full.at[pl.ds(src, 256), pl.ds(0, 1024)], query.at[pl.ds(dst, 256)], sem.at[0]))
             for q in range(4):
-                out = (key, value)[q % 2]
                 copies.append(pltpu.make_async_copy(
                     full.at[pl.ds(src + q * UNIT, UNIT), pl.ds(1024, 128)],
-                    out.at[:, pl.ds(dst + 128 * (q // 2), 128)],
-                    sem.at[n],
+                    (key, value)[q % 2].at[:, pl.ds(dst + 128 * (q // 2), 128)],
+                    sem.at[0],
                 ))
-                n += 1
     for copy in copies:
         copy.start()
-    scale_k[...] = total[:, 1024:1088]
-    scale_v[...] = total[:, 1088:1152]
-    for copy in copies:
+    near_k[...] = total[:, 1024:1088]
+    near_v[...] = total[:, 1088:1152]
+    thin = [pltpu.make_async_copy(near_k, scale_k, sem.at[2]), pltpu.make_async_copy(near_v, scale_v, sem.at[3])]
+    for copy in thin:
+        copy.start()
+    for copy in thin:
         copy.wait()
+    pltpu.make_async_copy(total.at[:, pl.ds(0, 1024)], scale_q, sem.at[1]).wait()
+    pltpu.make_async_copy(full, full, sem.at[0]).wait()
 
 
 def local(one_query, other_query, one_key, other_key, one_value, other_value, mix_share, norm_gain):
@@ -236,22 +235,17 @@
         in_specs=[hbm] * 8,
         out_specs=(vmem, vmem),
         scratch_shapes=[
-            pltpu.VMEM((256, 1024), f32),
-            pltpu.VMEM((256, 1024), f32),
-            pltpu.VMEM((128, 256), f32),
-            pltpu.VMEM((128, 256), f32),
-            pltpu.VMEM((1, 256), f32),
-            pltpu.VMEM((1, 256), f32),
+            pltpu.VMEM((2, 256, 1024), f32),
+            pltpu.VMEM((2, 128, 256), f32),
+            pltpu.VMEM((2, 1, 256), f32),
             pltpu.VMEM((256, 1152), f32),
             pltpu.VMEM((1, 1152), f32),
             pltpu.VMEM((8, 1, 1152), f32),
             pltpu.VMEM((1, 1152), f32),
             pltpu.VMEM((4, 1, 1152), f32),
-            pltpu.SemaphoreType.DMA((10,)),
-            pltpu.SemaphoreType.DMA((7,)),
-            pltpu.SemaphoreType.DMA((7,)),
-            pltpu.SemaphoreType.DMA((3,)),
-            pltpu.SemaphoreType.DMA((3,)),
+            pltpu.SemaphoreType.DMA((4,)),
+            pltpu.SemaphoreType.DMA((2,)),
+            pltpu.SemaphoreType.DMA((2,)),
             pltpu.SemaphoreType.DMA,
             pltpu.SemaphoreType.DMA((4, STEPS)),
             pltpu.SemaphoreType.DMA,
@@ -278,8 +272,8 @@
             jax.ShapeDtypeStruct((1, 64), f32),
         ),
         in_specs=[vmem, vmem],
-        out_specs=[hbm] * 4 + [vmem] * 2,
-        scratch_shapes=[pltpu.SemaphoreType.DMA((1 + 5 * 32,))],
+        out_specs=[hbm] * 6,
+        scratch_shapes=[pltpu.VMEM((1, 64), f32), pltpu.VMEM((1, 64), f32), pltpu.SemaphoreType.DMA((4,))],
         compiler_params=pltpu.CompilerParams(vmem_limit_bytes=4 * 2**20),
         name="write",
     )(full, total)

time: 73.6 us -> 71.4 us (0.970)
  Pallas kernels: 72.8 us -> 70.7 us
    pallas_call x1, Pallas kernels: 8.36 us -> 6.43 us  [local(): pl.pallas_call(write_kernel, out_shape=(jax.ShapeDtypeStruct((8192, 1024)...]
where the time goes in v2:
time: 71.4 us; the launch traced here: 71.3 us
  Pallas kernels  70.7 us (99%)
    pallas_call x1, Pallas kernels, local(): pl.pallas_call(gather_kernel, out_shape=(pltpu.VMEM((8192, 1152), bf16),...  64.2 us
    pallas_call x1, Pallas kernels, local(): pl.pallas_call(write_kernel, out_shape=(jax.ShapeDtypeStruct((8192, 1024)...  6.43 us

profile of v2, /device:TPU:1, one launch (start us, length us, event | category | flops | bytes accessed | tf_op | source)
XLA Modules:
  0.0 71.3 jit_solution(9616101041287612292)
XLA Ops:
  0.6 64.2 %gather.1 = (bf16[8192,1152]{1,0:T(8,128)(2,1)S(1)}, f32[1,1152]{1,0:T(1,128)S(1)}) custom-call(f32[256,1024]{1,0:T(8,128)} %one_q.1, f32[256,1024]{1,0:T(8,128)} %other_q.1, f32[64,256]{1,0:T(8,128)} %bitcast.11, f32[64,256]{1,0:T(8,128)} %bitcast.12, f32[64,256]{1,0:T(8,128)} %bitcast.13, f32[64,256]{1,0:T(8,128)} %bitcast.14, f32[1,256]{1,0:T(1,128)} %bitcast.15, ...), custom_call_target="tpu_custom_call" | custom-call | tf_op jit(solution)/shard_map/gather/pallas_call | solution.py:232
  64.9 6.4 %write.1 = (bf16[8192,1024]{1,0:T(8,128)(2,1)}, bf16[64,8192]{1,0:T(8,128)(2,1)}, bf16[64,8192]{1,0:T(8,128)(2,1)}, f32[1,1024]{1,0:T(1,128)}, f32[1,64]{1,0:T(1,128)}, /*index=5*/f32[1,64]{1,0:T(1,128)}) custom-call(bf16[8192,1152]{1,0:T(8,128)(2,1)S(1)} %get-tuple-element.14.full, f32[1,1152]{1,0:T(1,128)S(1)} %get-tuple-element.15.total), custom_call_target="tpu_custom_call" | custom-call | tf_op jit(solution)/shard_map/write/pallas_call | solution.py:264

commit v3 on v2

--- a/solution.py
+++ b/solution.py
@@ -41,6 +41,7 @@
 
 
 STEPS = len(PLUS_X)
+EARLY = ((0, 32), (32, 32))
 ARRIVAL = {received(link, slot): slot for link in range(4) for slot in range(STEPS)}
 
 
@@ -53,8 +54,8 @@
     one_q, other_q, one_k, other_k, one_v, other_v, mix, gain,
     full, total,
     in_q, in_kv, in_vec,
-    gained, part, row_sums, mid, col_sums,
-    load_sem, sum_send, sum_recv, send_sem, recv_sem, pair_recv,
+    gained, part, row_sums, mid, col_sums, early_in,
+    load_sem, sum_send, sum_recv, early_send, early_recv, send_sem, recv_sem, pair_recv,
 ):
     me = lax.axis_index("rows")
     core = lax.rem(me, NC)
@@ -117,12 +118,23 @@
     part[:, pl.ds(0, 1024)] = jnp.sum(sums, axis=0, keepdims=True)
 
     pl.semaphore_wait(barrier, len(row_peers) + len(col_peers))
+    def early(link, lo, count):
+        sx, sy, items = LINKS[link]
+        pltpu.make_async_remote_copy(
+            src_ref=gained.at[pl.ds(items[0][2] * UNIT + lo, count)], dst_ref=early_in.at[link, pl.ds(lo, count)],
+            send_sem=early_send, recv_sem=early_recv, device_id=device(sx, sy, core), device_id_type=MESH,
+        ).start()
+
     own = x * NC + core
     for dx, dy, c in row_peers:
         pltpu.make_async_remote_copy(
             src_ref=part, dst_ref=row_sums.at[own], send_sem=sum_send.at[0],
             recv_sem=sum_recv.at[0], device_id=device(dx, dy, c), device_id_type=MESH,
         ).start()
+    for link in (0, 1):
+        early(link, 0, UNIT)
+    for link in (2, 3):
+        early(link, *EARLY[0])
     row_sums[own] = part[...]
     others = row_sums.at[pl.ds(0, len(row_peers))]
     pltpu.make_async_copy(others, others, sum_recv.at[0]).wait()
@@ -135,6 +147,8 @@
             src_ref=mid, dst_ref=col_sums.at[y], send_sem=sum_send.at[1],
             recv_sem=sum_recv.at[1], device_id=device(dx, dy, c), device_id_type=MESH,
         ).start()
+    for link in (2, 3):
+        early(link, *EARLY[1])
     col_sums[y] = mid[...]
     others = col_sums.at[pl.ds(0, len(col_peers))]
     pltpu.make_async_copy(others, others, sum_recv.at[1]).wait()
@@ -154,7 +168,7 @@
         rows = rows_of(*items[slot])
         pltpu.make_async_remote_copy(
             src_ref=full.at[rows], dst_ref=full.at[rows], send_sem=send_sem,
-            recv_sem=recv_sem.at[link, slot], device_id=device(sx, sy, core), device_id_type=MESH,
+            recv_sem=recv_sem.at[slot - 1], device_id=device(sx, sy, core), device_id_type=MESH,
         ).start()
 
     def share(dx, dy, q):
@@ -164,24 +178,26 @@
             recv_sem=pair_recv, device_id=device(0, 0, 1 - core), device_id_type=MESH,
         ).start()
 
+    def finish(dst, q, value):
+        half = (q % 2) * UNIT
+        full[dst, pl.ds(0, 1024)] = (value[:, :1024] * inverse[:, :1024]).astype(jnp.bfloat16)
+        full[dst, pl.ds(1024, 128)] = (value[:, 1024:] * inverse_kv[half : half + UNIT]).astype(jnp.bfloat16)
+
     for q in range(4):
-        rows = pl.ds(q * UNIT, UNIT)
-        dst = rows_of(0, 0, q)
-        full[dst, pl.ds(0, 1024)] = (gained[rows, pl.ds(0, 1024)] * inverse[:, :1024]).astype(jnp.bfloat16)
-        half = (q % 2) * UNIT
-        full[dst, pl.ds(1024, 128)] = (gained[rows, pl.ds(1024, 128)] * inverse_kv[half : half + UNIT]).astype(jnp.bfloat16)
-
-    sent = [0, 0, 0, 0]
+        finish(rows_of(0, 0, q), q, gained[pl.ds(q * UNIT, UNIT), :])
+
+    sent = [1, 1, 1, 1]
     for slot in range(-1, STEPS):
-        if slot >= 0:
-            for link in range(4):
-                dx, dy, q = received(link, slot)
-                rows = rows_of(dx, dy, q)
-                pltpu.make_async_remote_copy(
-                    src_ref=full.at[rows], dst_ref=full.at[rows], send_sem=send_sem,
-                    recv_sem=recv_sem.at[link, slot], device_id=device(0, 0, 1 - core), device_id_type=MESH,
-                ).wait_recv()
-                share(dx, dy, q)
+        if slot == 0:
+            pltpu.make_async_copy(early_in, early_in, early_recv).wait()
+        elif slot > 0:
+            four = pl.ds(0, 4 * UNIT)
+            pltpu.make_async_copy(full.at[four], full.at[four], recv_sem.at[slot - 1]).wait()
+        for link in range(4 if slot >= 0 else 0):
+            dx, dy, q = received(link, slot)
+            if slot == 0:
+                finish(rows_of(dx, dy, q), q, early_in[link])
+            share(dx, dy, q)
         for link in range(4):
             while sent[link] < STEPS and due(link, sent[link]) <= slot:
                 send(link, sent[link])
@@ -192,8 +208,9 @@
 
     other = pl.ds(pl.multiple_of((1 - core) * 4096, 4096), 4096)
     pltpu.make_async_copy(full.at[other], full.at[other], pair_recv).wait()
-    everything = pl.ds(0, (4 * STEPS + 64) * UNIT)
+    everything = pl.ds(0, (4 * (STEPS - 1) + 64) * UNIT)
     pltpu.make_async_copy(full.at[everything], full.at[everything], send_sem).wait()
+    pltpu.make_async_copy(gained, gained, early_send).wait()
     sums_sent = row_sums.at[pl.ds(0, len(row_peers))]
     pltpu.make_async_copy(sums_sent, sums_sent, sum_send.at[0]).wait()
     sums_sent = col_sums.at[pl.ds(0, len(col_peers))]
@@ -243,11 +260,14 @@
             pltpu.VMEM((8, 1, 1152), f32),
             pltpu.VMEM((1, 1152), f32),
             pltpu.VMEM((4, 1, 1152), f32),
+            pltpu.VMEM((4, UNIT, 1152), f32),
             pltpu.SemaphoreType.DMA((4,)),
             pltpu.SemaphoreType.DMA((2,)),
             pltpu.SemaphoreType.DMA((2,)),
             pltpu.SemaphoreType.DMA,
-            pltpu.SemaphoreType.DMA((4, STEPS)),
+            pltpu.SemaphoreType.DMA,
+            pltpu.SemaphoreType.DMA,
+            pltpu.SemaphoreType.DMA((STEPS - 1,)),
             pltpu.SemaphoreType.DMA,
         ],
         compiler_params=pltpu.CompilerParams(

time: 71.4 us -> 68.9 us (0.965)
  Pallas kernels: 70.7 us -> 68.1 us
    pallas_call x1, Pallas kernels: 64.2 us -> 61.7 us  [local(): pl.pallas_call(gather_kernel, out_shape=(pltpu.VMEM((8192, 1152), bf16),...]
where the time goes in v3:
time: 68.9 us; the launch traced here: 68.8 us
  Pallas kernels  68.1 us (99%)
    pallas_call x1, Pallas kernels, local(): pl.pallas_call(gather_kernel, out_shape=(pltpu.VMEM((8192, 1152), bf16),...  61.7 us
    pallas_call x1, Pallas kernels, local(): pl.pallas_call(write_kernel, out_shape=(jax.ShapeDtypeStruct((8192, 1024)...  6.43 us

profile of v3, /device:TPU:1, one launch (start us, length us, event | category | flops | bytes accessed | tf_op | source)
XLA Modules:
  0.0 68.8 jit_solution(2403975123920943932)
XLA Ops:
  0.6 61.7 %gather.1 = (bf16[8192,1152]{1,0:T(8,128)(2,1)S(1)}, f32[1,1152]{1,0:T(1,128)S(1)}) custom-call(f32[256,1024]{1,0:T(8,128)} %one_q.1, f32[256,1024]{1,0:T(8,128)} %other_q.1, f32[64,256]{1,0:T(8,128)} %bitcast.11, f32[64,256]{1,0:T(8,128)} %bitcast.12, f32[64,256]{1,0:T(8,128)} %bitcast.13, f32[64,256]{1,0:T(8,128)} %bitcast.14, f32[1,256]{1,0:T(1,128)} %bitcast.15, ...), custom_call_target="tpu_custom_call" | custom-call | tf_op jit(solution)/shard_map/gather/pallas_call | solution.py:249
  62.3 6.4 %write.1 = (bf16[8192,1024]{1,0:T(8,128)(2,1)}, bf16[64,8192]{1,0:T(8,128)(2,1)}, bf16[64,8192]{1,0:T(8,128)(2,1)}, f32[1,1024]{1,0:T(1,128)}, f32[1,64]{1,0:T(1,128)}, /*index=5*/f32[1,64]{1,0:T(1,128)}) custom-call(bf16[8192,1152]{1,0:T(8,128)(2,1)S(1)} %get-tuple-element.14.full, f32[1,1152]{1,0:T(1,128)S(1)} %get-tuple-element.15.total), custom_call_target="tpu_custom_call" | custom-call | tf_op jit(solution)/shard_map/write/pallas_call | solution.py:284

commit v4 on v3

--- a/solution.py
+++ b/solution.py
@@ -41,6 +41,8 @@
 
 
 STEPS = len(PLUS_X)
+PIECES = [((0, UNIT),)] * (STEPS - 1) + [((0, 32), (32, 16), (48, 16))]
+FLAG = [sum(len(p) for p in PIECES[1:slot]) for slot in range(STEPS + 1)]
 EARLY = ((0, 32), (32, 32))
 ARRIVAL = {received(link, slot): slot for link in range(4) for slot in range(STEPS)}
 
@@ -69,12 +71,8 @@
     def device(dx, dy, c):
         return {"rows": at(dx, dy) * NC + c}
 
-    row_peers = [(1, 0, core), (3, 0, core), (2, 0, core), (1, 0, 1 - core), (3, 0, 1 - core), (2, 0, 1 - core), (0, 0, 1 - core)]
-    col_peers = [(0, 1, core), (0, 3, core), (0, 2, core)]
-    barrier = pltpu.get_barrier_semaphore()
-    for peer in row_peers + col_peers:
-        pl.semaphore_signal(barrier, inc=1, device_id=device(*peer), device_id_type=MESH)
-
+    row_peers = [(2, 0, core), (2, 0, 1 - core), (1, 0, core), (3, 0, core), (1, 0, 1 - core), (3, 0, 1 - core), (0, 0, 1 - core)]
+    col_peers = [(0, 2, core), (0, 1, core), (0, 3, core)]
     small = [
         pltpu.make_async_copy(mix, in_vec.at[0], load_sem.at[0]),
         pltpu.make_async_copy(gain, in_vec.at[1], load_sem.at[0]),
@@ -92,6 +90,9 @@
         wide.append(pltpu.make_async_copy(other_q.at[rows], in_q.at[1, rows], load_sem.at[2 + h]))
     for copy in small + thin + wide:
         copy.start()
+    barrier = pltpu.get_barrier_semaphore()
+    for peer in row_peers + col_peers:
+        pl.semaphore_signal(barrier, inc=1, device_id=device(*peer), device_id_type=MESH)
     pltpu.make_async_copy(in_vec, in_vec, load_sem.at[0]).wait()
     pltpu.make_async_copy(in_kv, in_kv, load_sem.at[1]).wait()
 
@@ -160,19 +161,20 @@
     inverse = 1.0 / scale
     inverse_kv = jnp.transpose(jnp.broadcast_to(inverse[:, 1024:], (128, 128)))
 
-    def rows_of(dx, dy, q):
-        return pl.ds(pl.multiple_of((core * NX * NY + at(dx, dy)) * 256 + q * UNIT, UNIT), UNIT)
+    def rows_of(dx, dy, q, lo=0, count=UNIT):
+        return pl.ds(pl.multiple_of((core * NX * NY + at(dx, dy)) * 256 + q * UNIT + lo, 16), count)
 
     def send(link, slot):
         sx, sy, items = LINKS[link]
-        rows = rows_of(*items[slot])
-        pltpu.make_async_remote_copy(
-            src_ref=full.at[rows], dst_ref=full.at[rows], send_sem=send_sem,
-            recv_sem=recv_sem.at[slot - 1], device_id=device(sx, sy, core), device_id_type=MESH,
-        ).start()
-
-    def share(dx, dy, q):
-        rows = rows_of(dx, dy, q)
+        for piece, (lo, count) in enumerate(PIECES[slot]):
+            rows = rows_of(*items[slot], lo, count)
+            pltpu.make_async_remote_copy(
+                src_ref=full.at[rows], dst_ref=full.at[rows], send_sem=send_sem,
+                recv_sem=recv_sem.at[FLAG[slot] + piece], device_id=device(sx, sy, core), device_id_type=MESH,
+            ).start()
+
+    def share(dx, dy, q, lo=0, count=UNIT):
+        rows = rows_of(dx, dy, q, lo, count)
         pltpu.make_async_remote_copy(
             src_ref=full.at[rows], dst_ref=full.at[rows], send_sem=send_sem,
             recv_sem=pair_recv, device_id=device(0, 0, 1 - core), device_id_type=MESH,
@@ -190,14 +192,16 @@
     for slot in range(-1, STEPS):
         if slot == 0:
             pltpu.make_async_copy(early_in, early_in, early_recv).wait()
+            for link in range(4):
+                dx, dy, q = received(link, slot)
+                finish(rows_of(dx, dy, q), q, early_in[link])
+                share(dx, dy, q)
         elif slot > 0:
-            four = pl.ds(0, 4 * UNIT)
-            pltpu.make_async_copy(full.at[four], full.at[four], recv_sem.at[slot - 1]).wait()
-        for link in range(4 if slot >= 0 else 0):
-            dx, dy, q = received(link, slot)
-            if slot == 0:
-                finish(rows_of(dx, dy, q), q, early_in[link])
-            share(dx, dy, q)
+            for piece, (lo, count) in enumerate(PIECES[slot]):
+                four = pl.ds(0, 4 * count)
+                pltpu.make_async_copy(full.at[four], full.at[four], recv_sem.at[FLAG[slot] + piece]).wait()
+                for link in range(4):
+                    share(*received(link, slot), lo, count)
         for link in range(4):
             while sent[link] < STEPS and due(link, sent[link]) <= slot:
                 send(link, sent[link])
@@ -267,7 +271,7 @@
             pltpu.SemaphoreType.DMA,
             pltpu.SemaphoreType.DMA,
             pltpu.SemaphoreType.DMA,
-            pltpu.SemaphoreType.DMA((STEPS - 1,)),
+            pltpu.SemaphoreType.DMA((FLAG[STEPS],)),
             pltpu.SemaphoreType.DMA,
         ],
         compiler_params=pltpu.CompilerParams(

time: 68.9 us -> 68 us (0.987)
  Pallas kernels: 68.1 us -> 67.3 us
    pallas_call x1, Pallas kernels: 61.7 us -> 60.9 us  [local(): pl.pallas_call(gather_kernel, out_shape=(pltpu.VMEM((8192, 1152), bf16),...]
where the time goes in v4:
time: 68 us; the launch traced here: 67.9 us
  Pallas kernels  67.3 us (99%)
    pallas_call x1, Pallas kernels, local(): pl.pallas_call(gather_kernel, out_shape=(pltpu.VMEM((8192, 1152), bf16),...  60.9 us
    pallas_call x1, Pallas kernels, local(): pl.pallas_call(write_kernel, out_shape=(jax.ShapeDtypeStruct((8192, 1024)...  6.43 us

profile of v4, /device:TPU:1, one launch (start us, length us, event | category | flops | bytes accessed | tf_op | source)
XLA Modules:
  0.0 67.9 jit_solution(12000299154586922888)
XLA Ops:
  0.6 60.9 %gather.1 = (bf16[8192,1152]{1,0:T(8,128)(2,1)S(1)}, f32[1,1152]{1,0:T(1,128)S(1)}) custom-call(f32[256,1024]{1,0:T(8,128)} %one_q.1, f32[256,1024]{1,0:T(8,128)} %other_q.1, f32[64,256]{1,0:T(8,128)} %bitcast.11, f32[64,256]{1,0:T(8,128)} %bitcast.12, f32[64,256]{1,0:T(8,128)} %bitcast.13, f32[64,256]{1,0:T(8,128)} %bitcast.14, f32[1,256]{1,0:T(1,128)} %bitcast.15, ...), custom_call_target="tpu_custom_call" | custom-call | tf_op jit(solution)/shard_map/gather/pallas_call | solution.py:253
  61.5 6.4 %write.1 = (bf16[8192,1024]{1,0:T(8,128)(2,1)}, bf16[64,8192]{1,0:T(8,128)(2,1)}, bf16[64,8192]{1,0:T(8,128)(2,1)}, f32[1,1024]{1,0:T(1,128)}, f32[1,64]{1,0:T(1,128)}, /*index=5*/f32[1,64]{1,0:T(1,128)}) custom-call(bf16[8192,1152]{1,0:T(8,128)(2,1)S(1)} %get-tuple-element.14.full, f32[1,1152]{1,0:T(1,128)S(1)} %get-tuple-element.15.total), custom_call_target="tpu_custom_call" | custom-call | tf_op jit(solution)/shard_map/write/pallas_call | solution.py:288

commit v5 on v3

--- a/solution.py
+++ b/solution.py
@@ -41,6 +41,12 @@
 
 
 STEPS = len(PLUS_X)
+PIECES = [((0, UNIT),)] * (STEPS - 1) + [((0, 32), (32, 16), (48, 16))]
+FLAG = [sum(len(p) for p in PIECES[1:slot]) for slot in range(STEPS + 1)]
+SPLIT = (12, 6)
+READY = 10
+PACE = 10
+FIRST = SPLIT.index(min(SPLIT))
 EARLY = ((0, 32), (32, 32))
 ARRIVAL = {received(link, slot): slot for link in range(4) for slot in range(STEPS)}
 
@@ -69,12 +75,8 @@
     def device(dx, dy, c):
         return {"rows": at(dx, dy) * NC + c}
 
-    row_peers = [(1, 0, core), (3, 0, core), (2, 0, core), (1, 0, 1 - core), (3, 0, 1 - core), (2, 0, 1 - core), (0, 0, 1 - core)]
-    col_peers = [(0, 1, core), (0, 3, core), (0, 2, core)]
-    barrier = pltpu.get_barrier_semaphore()
-    for peer in row_peers + col_peers:
-        pl.semaphore_signal(barrier, inc=1, device_id=device(*peer), device_id_type=MESH)
-
+    row_peers = [(2, 0, core), (2, 0, 1 - core), (1, 0, core), (3, 0, core), (1, 0, 1 - core), (3, 0, 1 - core), (0, 0, 1 - core)]
+    col_peers = [(0, 2, core), (0, 1, core), (0, 3, core)]
     small = [
         pltpu.make_async_copy(mix, in_vec.at[0], load_sem.at[0]),
         pltpu.make_async_copy(gain, in_vec.at[1], load_sem.at[0]),
@@ -92,6 +94,9 @@
         wide.append(pltpu.make_async_copy(other_q.at[rows], in_q.at[1, rows], load_sem.at[2 + h]))
     for copy in small + thin + wide:
         copy.start()
+    barrier = pltpu.get_barrier_semaphore()
+    for peer in row_peers + col_peers:
+        pl.semaphore_signal(barrier, inc=1, device_id=device(*peer), device_id_type=MESH)
     pltpu.make_async_copy(in_vec, in_vec, load_sem.at[0]).wait()
     pltpu.make_async_copy(in_kv, in_kv, load_sem.at[1]).wait()
 
@@ -168,7 +173,7 @@
         rows = rows_of(*items[slot])
         pltpu.make_async_remote_copy(
             src_ref=full.at[rows], dst_ref=full.at[rows], send_sem=send_sem,
-            recv_sem=recv_sem.at[slot - 1], device_id=device(sx, sy, core), device_id_type=MESH,
+            recv_sem=recv_sem.at[slot], device_id=device(sx, sy, core), device_id_type=MESH,
         ).start()
 
     def share(dx, dy, q):
@@ -186,30 +191,35 @@
     for q in range(4):
         finish(rows_of(0, 0, q), q, gained[pl.ds(q * UNIT, UNIT), :])
 
-    sent = [1, 1, 1, 1]
-    for slot in range(-1, STEPS):
-        if slot == 0:
-            pltpu.make_async_copy(early_in, early_in, early_recv).wait()
-        elif slot > 0:
-            four = pl.ds(0, 4 * UNIT)
-            pltpu.make_async_copy(full.at[four], full.at[four], recv_sem.at[slot - 1]).wait()
-        for link in range(4 if slot >= 0 else 0):
-            dx, dy, q = received(link, slot)
+    def run(c):
+        sent = [1, 1, 1, 1]
+        for slot in range(-1, SPLIT[c]):
             if slot == 0:
-                finish(rows_of(dx, dy, q), q, early_in[link])
-            share(dx, dy, q)
-        for link in range(4):
-            while sent[link] < STEPS and due(link, sent[link]) <= slot:
-                send(link, sent[link])
-                sent[link] += 1
-        if slot == -1:
-            for q in range(4):
-                share(0, 0, q)
-
-    other = pl.ds(pl.multiple_of((1 - core) * 4096, 4096), 4096)
-    pltpu.make_async_copy(full.at[other], full.at[other], pair_recv).wait()
-    everything = pl.ds(0, (4 * (STEPS - 1) + 64) * UNIT)
-    pltpu.make_async_copy(full.at[everything], full.at[everything], send_sem).wait()
+                pltpu.make_async_copy(early_in, early_in, early_recv).wait()
+                for link in range(4):
+                    dx, dy, q = received(link, slot)
+                    finish(rows_of(dx, dy, q), q, early_in[link])
+                    share(dx, dy, q)
+            elif slot > 0:
+                four = pl.ds(0, 4 * UNIT)
+                pltpu.make_async_copy(full.at[four], full.at[four], recv_sem.at[slot]).wait()
+                if slot < min(SPLIT):
+                    for link in range(4):
+                        share(*received(link, slot))
+            for link in range(4):
+                while sent[link] < SPLIT[c] and due(link, sent[link]) <= slot:
+                    send(link, sent[link])
+                    sent[link] += 1
+            if slot == -1:
+                for q in range(4):
+                    share(0, 0, q)
+        other = pl.ds(0, (4 + 4 * min(SPLIT)) * UNIT)
+        pltpu.make_async_copy(full.at[other], full.at[other], pair_recv).wait()
+        everything = pl.ds(0, (4 * (SPLIT[c] - 1) + 4 + 4 * min(SPLIT)) * UNIT)
+        pltpu.make_async_copy(full.at[everything], full.at[everything], send_sem).wait()
+
+    for c in range(NC):
+        pl.when(core == c)(functools.partial(run, c))
     pltpu.make_async_copy(gained, gained, early_send).wait()
     sums_sent = row_sums.at[pl.ds(0, len(row_peers))]
     pltpu.make_async_copy(sums_sent, sums_sent, sum_send.at[0]).wait()
@@ -217,36 +227,143 @@
     pltpu.make_async_copy(sums_sent, sums_sent, sum_send.at[1]).wait()
 
 
-def write_kernel(full, total, query, key, value, scale_q, scale_k, scale_v, near_k, near_v, sem):
-    copies = [pltpu.make_async_copy(total.at[:, pl.ds(0, 1024)], scale_q, sem.at[1])]
+def rest_kernel(first, token, full, send_sem, recv_sem, pair_recv, ready):
+    me = lax.axis_index("rows")
+    core = lax.rem(me, NC)
+    chip = lax.div(me, NC)
+    x = lax.rem(chip, NX)
+    y = lax.div(chip, NX)
+
+    def at(dx, dy):
+        return lax.rem(y + dy % NY, NY) * NX + lax.rem(x + dx % NX, NX)
+
+    def device(dx, dy, c):
+        return {"rows": at(dx, dy) * NC + c}
+
+    barrier = pltpu.get_barrier_semaphore()
+    for sx, sy, _ in LINKS:
+        pl.semaphore_signal(barrier, inc=1, device_id=device(sx, sy, core), device_id_type=MESH)
+
+    def run(c):
+        if c == FIRST:
+            pl.semaphore_signal(barrier, inc=1, device_id=device(0, 0, 1 - FIRST), device_id_type=MESH)
+        pl.semaphore_wait(barrier, 4 if c == FIRST else 5)
+        if c != FIRST:
+            pl.semaphore_signal(ready, inc=1, device_id=device(0, 0, FIRST), device_id_type=MESH)
+
+        def rows_of(dx, dy, q, lo=0, count=UNIT):
+            return pl.ds(pl.multiple_of((c * NX * NY + at(dx, dy)) * 256 + q * UNIT + lo, 16), count)
+
+        def send(link, slot):
+            sx, sy, items = LINKS[link]
+            src = first if due(link, slot) < SPLIT[c] else full
+            for piece, (lo, count) in enumerate(PIECES[slot]):
+                rows = rows_of(*items[slot], lo, count)
+                pltpu.make_async_remote_copy(
+                    src_ref=src.at[rows], dst_ref=full.at[rows], send_sem=send_sem,
+                    recv_sem=recv_sem.at[FLAG[slot] - FLAG[min(SPLIT)] + piece],
+                    device_id=device(sx, sy, c), device_id_type=MESH,
+                ).start()
+
+        def share(src, dx, dy, q, lo=0, count=UNIT):
+            rows = rows_of(dx, dy, q, lo, count)
+            pltpu.make_async_remote_copy(
+                src_ref=src.at[rows], dst_ref=full.at[rows], send_sem=send_sem,
+                recv_sem=pair_recv, device_id=device(0, 0, 1 - c), device_id_type=MESH,
+            ).start()
+
+        sent = [SPLIT[c]] * 4
+        held = [(first, *received(link, slot)) for slot in range(min(SPLIT), SPLIT[c]) for link in range(4)]
+        for slot in range(SPLIT[c] - 1, STEPS):
+            if c == FIRST and slot == READY:
+                pl.semaphore_wait(ready, 1)
+            for piece, (lo, count) in enumerate(PIECES[slot] if slot >= SPLIT[c] else ()):
+                four = pl.ds(0, 4 * count)
+                pltpu.make_async_copy(
+                    full.at[four], full.at[four], recv_sem.at[FLAG[slot] - FLAG[min(SPLIT)] + piece]
+                ).wait()
+                for link in range(4):
+                    item = (full, *received(link, slot), lo, count)
+                    if c == FIRST and slot < READY:
+                        held.append(item)
+                    else:
+                        share(*item)
+            for link in range(4):
+                while sent[link] < STEPS and due(link, sent[link]) <= slot:
+                    send(link, sent[link])
+                    sent[link] += 1
+            if c != FIRST or slot >= READY:
+                for _ in range(min(PACE, len(held))):
+                    share(*held.pop(0))
+        assert not held
+        other = pl.ds(0, 4 * (STEPS - min(SPLIT)) * UNIT)
+        pltpu.make_async_copy(full.at[other], full.at[other], pair_recv).wait()
+        everything = pl.ds(0, (4 * (STEPS - SPLIT[c]) + 4 * (STEPS - min(SPLIT))) * UNIT)
+        pltpu.make_async_copy(full.at[everything], full.at[everything], send_sem).wait()
+
     for c in range(NC):
-        for p in range(NX * NY):
-            src, dst = (c * NX * NY + p) * 256, (p * NC + c) * 256
-            copies.append(pltpu.make_async_copy(full.at[pl.ds(src, 256), pl.ds(0, 1024)], query.at[pl.ds(dst, 256)], sem.at[0]))
-            for q in range(4):
-                copies.append(pltpu.make_async_copy(
-                    full.at[pl.ds(src + q * UNIT, UNIT), pl.ds(1024, 128)],
-                    (key, value)[q % 2].at[:, pl.ds(dst + 128 * (q // 2), 128)],
-                    sem.at[0],
-                ))
-    for copy in copies:
-        copy.start()
+        pl.when(core == c)(functools.partial(run, c))
+
+
+def write_units(full, query, key, value, sem, first):
+    me = lax.axis_index("rows")
+    core = lax.rem(me, NC)
+    chip = lax.div(me, NC)
+    x = lax.rem(chip, NX)
+    y = lax.div(chip, NX)
+
+    def run(c):
+        count = 0
+        for net in range(NC):
+            units = [(0, 0, q) for q in range(4)] if first else []
+            last = SPLIT[c] if net == c else min(SPLIT)
+            for slot in range(0, last) if first else range(last, STEPS):
+                units += [received(link, slot) for link in range(4)]
+            for dx, dy, q in units:
+                chip = lax.rem(y + dy % NY, NY) * NX + lax.rem(x + dx % NX, NX)
+                src = pl.ds(pl.multiple_of((net * NX * NY + chip) * 256 + q * UNIT, UNIT), UNIT)
+                dst = pl.multiple_of((chip * NC + net) * 256, 256)
+                pltpu.make_async_copy(
+                    full.at[src, pl.ds(0, 1024)], query.at[pl.ds(pl.multiple_of(dst + q * UNIT, UNIT), UNIT)], sem
+                ).start()
+                pltpu.make_async_copy(
+                    full.at[src, pl.ds(1024, 128)],
+                    (key, value)[q % 2].at[:, pl.ds(pl.multiple_of(dst + 128 * (q // 2), 128), 128)],
+                    sem,
+                ).start()
+            count += len(units)
+        everything = pl.ds(0, count * UNIT)
+        pltpu.make_async_copy(full.at[everything], full.at[everything], sem).wait()
+
+    for c in range(NC):
+        pl.when(core == c)(functools.partial(run, c))
+
+
+def write_first(full, total, query, key, value, scale_q, scale_k, scale_v, token, near_k, near_v, sem):
     near_k[...] = total[:, 1024:1088]
     near_v[...] = total[:, 1088:1152]
-    thin = [pltpu.make_async_copy(near_k, scale_k, sem.at[2]), pltpu.make_async_copy(near_v, scale_v, sem.at[3])]
+    thin = [
+        pltpu.make_async_copy(total.at[:, pl.ds(0, 1024)], scale_q, sem.at[1]),
+        pltpu.make_async_copy(near_k, scale_k, sem.at[2]),
+        pltpu.make_async_copy(near_v, scale_v, sem.at[3]),
+    ]
     for copy in thin:
         copy.start()
+    token[...] = jnp.zeros_like(token)
+    write_units(full, query, key, value, sem.at[0], True)
     for copy in thin:
         copy.wait()
-    pltpu.make_async_copy(total.at[:, pl.ds(0, 1024)], scale_q, sem.at[1]).wait()
-    pltpu.make_async_copy(full, full, sem.at[0]).wait()
+
+
+def write_rest(full, query_in, key_in, value_in, query, key, value, sem):
+    write_units(full, query, key, value, sem.at[0], False)
 
 
 def local(one_query, other_query, one_key, other_key, one_value, other_value, mix_share, norm_gain):
     hbm = pl.BlockSpec(memory_space=pltpu.HBM)
     vmem = pl.BlockSpec(memory_space=pltpu.VMEM)
     f32, bf16 = jnp.float32, jnp.bfloat16
-    full, total = pl.pallas_call(
+    first, total = pl.pallas_call(
         gather_kernel,
         out_shape=(pltpu.VMEM((8192, 1152), bf16), pltpu.VMEM((1, 1152), f32)),
         in_specs=[hbm] * 8,
@@ -267,11 +384,11 @@
             pltpu.SemaphoreType.DMA,
             pltpu.SemaphoreType.DMA,
             pltpu.SemaphoreType.DMA,
-            pltpu.SemaphoreType.DMA((STEPS - 1,)),
+            pltpu.SemaphoreType.DMA((max(SPLIT),)),
             pltpu.SemaphoreType.DMA,
         ],
         compiler_params=pltpu.CompilerParams(
-            collective_id=0, has_side_effects=True, vmem_limit_bytes=16 * 2**20
+            collective_id=0, has_side_effects=True, vmem_limit_bytes=10 * 2**20
         ),
         name="gather",
     )(*(
@@ -281,22 +398,49 @@
             mix_share.reshape(1, 256), norm_gain.reshape(1, 256),
         )
     ))
-    query, key, value, scale_q, scale_k, scale_v = pl.pallas_call(
-        write_kernel,
-        out_shape=(
-            jax.ShapeDtypeStruct((8192, 1024), bf16),
-            jax.ShapeDtypeStruct((64, 8192), bf16),
-            jax.ShapeDtypeStruct((64, 8192), bf16),
+    placed = (
+        jax.ShapeDtypeStruct((8192, 1024), bf16),
+        jax.ShapeDtypeStruct((64, 8192), bf16),
+        jax.ShapeDtypeStruct((64, 8192), bf16),
+    )
+    query, key, value, scale_q, scale_k, scale_v, token = pl.pallas_call(
+        write_first,
+        out_shape=placed + (
             jax.ShapeDtypeStruct((1, 1024), f32),
             jax.ShapeDtypeStruct((1, 64), f32),
             jax.ShapeDtypeStruct((1, 64), f32),
+            pltpu.VMEM((8, 128), f32),
         ),
         in_specs=[vmem, vmem],
-        out_specs=[hbm] * 6,
+        out_specs=[hbm] * 6 + [vmem],
         scratch_shapes=[pltpu.VMEM((1, 64), f32), pltpu.VMEM((1, 64), f32), pltpu.SemaphoreType.DMA((4,))],
-        compiler_params=pltpu.CompilerParams(vmem_limit_bytes=4 * 2**20),
-        name="write",
-    )(full, total)
+        compiler_params=pltpu.CompilerParams(vmem_limit_bytes=2 * 2**20),
+        name="write_first",
+    )(first, total)
+    rest = pl.pallas_call(
+        rest_kernel,
+        out_shape=pltpu.VMEM((8192, 1152), bf16),
+        in_specs=[vmem, vmem],
+        out_specs=vmem,
+        scratch_shapes=[
+            pltpu.SemaphoreType.DMA,
+            pltpu.SemaphoreType.DMA((FLAG[STEPS] - FLAG[min(SPLIT)],)),
+            pltpu.SemaphoreType.DMA,
+            pltpu.SemaphoreType.REGULAR,
+        ],
+        compiler_params=pltpu.CompilerParams(collective_id=1, has_side_effects=True, vmem_limit_bytes=2 * 2**20),
+        name="rest",
+    )(first, token)
+    query, key, value = pl.pallas_call(
+        write_rest,
+        out_shape=placed,
+        in_specs=[vmem, hbm, hbm, hbm],
+        out_specs=[hbm] * 3,
+        input_output_aliases={1: 0, 2: 1, 3: 2},
+        scratch_shapes=[pltpu.SemaphoreType.DMA((1,))],
+        compiler_params=pltpu.CompilerParams(vmem_limit_bytes=2 * 2**20),
+        name="write_rest",
+    )(rest, query, key, value)
     return (query, key.T, value.T, scale_q.reshape(1024), scale_k.reshape(64), scale_v.reshape(64))
 
 

time: 68.9 us -> 65.5 us (0.951)
  Pallas kernels: 68.1 us -> 64.7 us
    pallas_call x1, Pallas kernels: 61.7 us -> 33 us  [local(): pl.pallas_call(gather_kernel, out_shape=(pltpu.VMEM((8192, 1152), bf16),...]
    pallas_call x1 -> x3, Pallas kernels: 6.43 us -> 31.7 us  [the longest x1 24.5 us: local(): pl.pallas_call(rest_kernel, out_shape=pltpu.VMEM((8192, 1152), bf16), in_...]
where the time goes in v5:
time: 65.5 us; the launch traced here: 65.4 us
  Pallas kernels  64.7 us (99%)
  between operations  0.66 us (1%)
    pallas_call x1, Pallas kernels, local(): pl.pallas_call(gather_kernel, out_shape=(pltpu.VMEM((8192, 1152), bf16),...  33 us
    pallas_call x1, Pallas kernels, local(): pl.pallas_call(rest_kernel, out_shape=pltpu.VMEM((8192, 1152), bf16), in_...  24.5 us
    pallas_call x1, Pallas kernels, local(): pl.pallas_call(write_rest, out_shape=placed, in_specs=[vmem, hbm, hbm, hb...  3.93 us
    pallas_call x1, Pallas kernels, local(): pl.pallas_call(write_first, out_shape=placed + (jax.ShapeDtypeStruct((1,...  3.3 us

profile of v5, /device:TPU:1, one launch (start us, length us, event | category | flops | bytes accessed | tf_op | source)
XLA Modules:
  0.0 65.4 jit_solution(5820238762573033138)
XLA Ops:
  0.6 33.0 %gather.1 = (bf16[8192,1152]{1,0:T(8,128)(2,1)S(1)}, f32[1,1152]{1,0:T(1,128)S(1)}) custom-call(f32[256,1024]{1,0:T(8,128)} %one_q.1, f32[256,1024]{1,0:T(8,128)} %other_q.1, f32[64,256]{1,0:T(8,128)} %bitcast.13, f32[64,256]{1,0:T(8,128)} %bitcast.14, f32[64,256]{1,0:T(8,128)} %bitcast.15, f32[64,256]{1,0:T(8,128)} %bitcast.16, f32[1,256]{1,0:T(1,128)} %bitcast.17, ...), custom_call_target="tpu_custom_call" | custom-call | tf_op jit(solution)/shard_map/gather/pallas_call | solution.py:366
  33.7 3.3 %write_first.1 = (bf16[8192,1024]{1,0:T(8,128)(2,1)}, bf16[64,8192]{1,0:T(8,128)(2,1)}, bf16[64,8192]{1,0:T(8,128)(2,1)}, f32[1,1024]{1,0:T(1,128)}, f32[1,64]{1...) custom-call(bf16[8192,1152]{1,0:T(8,128)(2,1)S(1)} %get-tuple-element.18.full.first, ...), custom_call_target="tpu_custom_call" | custom-call | tf_op jit(solution)/shard_map/write_first/pallas_call | solution.py:406
  37.0 24.5 %rest.1.full = bf16[8192,1152]{1,0:T(8,128)(2,1)S(1)} custom-call(bf16[8192,1152]{1,0:T(8,128)(2,1)S(1)} %get-tuple-element.18.full.first, f32[8,128]{1,0:T(8,128)S(1)} %get-tuple-element.20.token), custom_call_target="tpu_custom_call" | custom-call | tf_op jit(solution)/shard_map/rest/pallas_call | solution.py:420
  61.4 3.9 %write_rest.1 = (bf16[8192,1024]{1,0:T(8,128)(2,1)}, bf16[64,8192]{1,0:T(8,128)(2,1)}, bf16[64,8192]{1,0:T(8,128)(2,1)}) custom-call(bf16[8192,1152]{1,0:T(8,128)(2,1)S(1)} %rest.1.full, bf16[8192,1024]{1,0:T(8,128)(2,1)} %get-tuple-element.21.query_in, ...), custom_call_target="tpu_custom_call", output_to_operand_aliasing={{0}: (1, {}), {1}: (2, {}), {2}: (3, {})} | custom-call | tf_op jit(solution)/shard_map/write_rest/pallas_call | solution.py:434

commit v6 on v5

--- a/solution.py
+++ b/solution.py
@@ -43,9 +43,9 @@
 STEPS = len(PLUS_X)
 PIECES = [((0, UNIT),)] * (STEPS - 1) + [((0, 32), (32, 16), (48, 16))]
 FLAG = [sum(len(p) for p in PIECES[1:slot]) for slot in range(STEPS + 1)]
-SPLIT = (12, 6)
-READY = 10
-PACE = 10
+SPLIT = (6, 13)
+READY = 11
+PACE = 40
 FIRST = SPLIT.index(min(SPLIT))
 EARLY = ((0, 32), (32, 32))
 ARRIVAL = {received(link, slot): slot for link in range(4) for slot in range(STEPS)}

time: 65.5 us -> 64.2 us (0.980)
  Pallas kernels: 64.7 us -> 63.4 us
    pallas_call x1, Pallas kernels: 24.5 us -> 13.9 us  [local(): pl.pallas_call(rest_kernel, out_shape=pltpu.VMEM((8192, 1152), bf16), in_...]
    pallas_call x1, Pallas kernels: 33 us -> 42.3 us  [local(): pl.pallas_call(gather_kernel, out_shape=(pltpu.VMEM((8192, 1152), bf16),...]
    pallas_call x1, Pallas kernels: 3.93 us -> 2.7 us  [local(): pl.pallas_call(write_rest, out_shape=placed, in_specs=[vmem, hbm, hbm, hb...]
    pallas_call x1, Pallas kernels: 3.3 us -> 4.52 us  [local(): pl.pallas_call(write_first, out_shape=placed + (jax.ShapeDtypeStruct((1,...]
where the time goes in v6:
time: 64.2 us; the launch traced here: 64.1 us
  Pallas kernels  63.4 us (99%)
  between operations  0.66 us (1%)
    pallas_call x1, Pallas kernels, local(): pl.pallas_call(gather_kernel, out_shape=(pltpu.VMEM((8192, 1152), bf16),...  42.3 us
    pallas_call x1, Pallas kernels, local(): pl.pallas_call(rest_kernel, out_shape=pltpu.VMEM((8192, 1152), bf16), in_...  13.9 us
    pallas_call x1, Pallas kernels, local(): pl.pallas_call(write_first, out_shape=placed + (jax.ShapeDtypeStruct((1,...  4.52 us
    pallas_call x1, Pallas kernels, local(): pl.pallas_call(write_rest, out_shape=placed, in_specs=[vmem, hbm, hbm, hb...  2.7 us

profile of v6, /device:TPU:1, one launch (start us, length us, event | category | flops | bytes accessed | tf_op | source)
XLA Modules:
  0.0 64.1 jit_solution(6487199723079559267)
XLA Ops:
  0.6 42.3 %gather.1 = (bf16[8192,1152]{1,0:T(8,128)(2,1)S(1)}, f32[1,1152]{1,0:T(1,128)S(1)}) custom-call(f32[256,1024]{1,0:T(8,128)} %one_q.1, f32[256,1024]{1,0:T(8,128)} %other_q.1, f32[64,256]{1,0:T(8,128)} %bitcast.13, f32[64,256]{1,0:T(8,128)} %bitcast.14, f32[64,256]{1,0:T(8,128)} %bitcast.15, f32[64,256]{1,0:T(8,128)} %bitcast.16, f32[1,256]{1,0:T(1,128)} %bitcast.17, ...), custom_call_target="tpu_custom_call" | custom-call | tf_op jit(solution)/shard_map/gather/pallas_call | solution.py:366
  42.9 4.5 %write_first.1 = (bf16[8192,1024]{1,0:T(8,128)(2,1)}, bf16[64,8192]{1,0:T(8,128)(2,1)}, bf16[64,8192]{1,0:T(8,128)(2,1)}, f32[1,1024]{1,0:T(1,128)}, f32[1,64]{1...) custom-call(bf16[8192,1152]{1,0:T(8,128)(2,1)S(1)} %get-tuple-element.18.full.first, ...), custom_call_target="tpu_custom_call" | custom-call | tf_op jit(solution)/shard_map/write_first/pallas_call | solution.py:406
  47.5 13.9 %rest.1.full = bf16[8192,1152]{1,0:T(8,128)(2,1)S(1)} custom-call(bf16[8192,1152]{1,0:T(8,128)(2,1)S(1)} %get-tuple-element.18.full.first, f32[8,128]{1,0:T(8,128)S(1)} %get-tuple-element.20.token), custom_call_target="tpu_custom_call" | custom-call | tf_op jit(solution)/shard_map/rest/pallas_call | solution.py:420
  61.4 2.7 %write_rest.1 = (bf16[8192,1024]{1,0:T(8,128)(2,1)}, bf16[64,8192]{1,0:T(8,128)(2,1)}, bf16[64,8192]{1,0:T(8,128)(2,1)}) custom-call(bf16[8192,1152]{1,0:T(8,128)(2,1)S(1)} %rest.1.full, bf16[8192,1024]{1,0:T(8,128)(2,1)} %get-tuple-element.21.query_in, ...), custom_call_target="tpu_custom_call", output_to_operand_aliasing={{0}: (1, {}), {1}: (2, {}), {2}: (3, {})} | custom-call | tf_op jit(solution)/shard_map/write_rest/pallas_call | solution.py:434

commit v7 on v6

--- a/solution.py
+++ b/solution.py
@@ -43,10 +43,11 @@
 STEPS = len(PLUS_X)
 PIECES = [((0, UNIT),)] * (STEPS - 1) + [((0, 32), (32, 16), (48, 16))]
 FLAG = [sum(len(p) for p in PIECES[1:slot]) for slot in range(STEPS + 1)]
-SPLIT = (6, 13)
+SPLIT = (7, 13)
 READY = 11
 PACE = 40
 FIRST = SPLIT.index(min(SPLIT))
+SHARED = min(SPLIT) - 1
 EARLY = ((0, 32), (32, 32))
 ARRIVAL = {received(link, slot): slot for link in range(4) for slot in range(STEPS)}
 
@@ -203,7 +204,7 @@
             elif slot > 0:
                 four = pl.ds(0, 4 * UNIT)
                 pltpu.make_async_copy(full.at[four], full.at[four], recv_sem.at[slot]).wait()
-                if slot < min(SPLIT):
+                if slot < SHARED:
                     for link in range(4):
                         share(*received(link, slot))
             for link in range(4):
@@ -213,9 +214,9 @@
             if slot == -1:
                 for q in range(4):
                     share(0, 0, q)
-        other = pl.ds(0, (4 + 4 * min(SPLIT)) * UNIT)
+        other = pl.ds(0, (4 + 4 * SHARED) * UNIT)
         pltpu.make_async_copy(full.at[other], full.at[other], pair_recv).wait()
-        everything = pl.ds(0, (4 * (SPLIT[c] - 1) + 4 + 4 * min(SPLIT)) * UNIT)
+        everything = pl.ds(0, (4 * (SPLIT[c] - 1) + 4 + 4 * SHARED) * UNIT)
         pltpu.make_async_copy(full.at[everything], full.at[everything], send_sem).wait()
 
     for c in range(NC):
@@ -273,7 +274,7 @@
             ).start()
 
         sent = [SPLIT[c]] * 4
-        held = [(first, *received(link, slot)) for slot in range(min(SPLIT), SPLIT[c]) for link in range(4)]
+        held = [(first, *received(link, slot)) for slot in range(SHARED, SPLIT[c]) for link in range(4)]
         for slot in range(SPLIT[c] - 1, STEPS):
             if c == FIRST and slot == READY:
                 pl.semaphore_wait(ready, 1)
@@ -296,9 +297,9 @@
                 for _ in range(min(PACE, len(held))):
                     share(*held.pop(0))
         assert not held
-        other = pl.ds(0, 4 * (STEPS - min(SPLIT)) * UNIT)
+        other = pl.ds(0, 4 * (STEPS - SHARED) * UNIT)
         pltpu.make_async_copy(full.at[other], full.at[other], pair_recv).wait()
-        everything = pl.ds(0, (4 * (STEPS - SPLIT[c]) + 4 * (STEPS - min(SPLIT))) * UNIT)
+        everything = pl.ds(0, (4 * (STEPS - SPLIT[c]) + 4 * (STEPS - SHARED)) * UNIT)
         pltpu.make_async_copy(full.at[everything], full.at[everything], send_sem).wait()
 
     for c in range(NC):
@@ -316,7 +317,7 @@
         count = 0
         for net in range(NC):
             units = [(0, 0, q) for q in range(4)] if first else []
-            last = SPLIT[c] if net == c else min(SPLIT)
+            last = SPLIT[c] if net == c else SHARED
             for slot in range(0, last) if first else range(last, STEPS):
                 units += [received(link, slot) for link in range(4)]
             for dx, dy, q in units:

time: 64.2 us -> 64.2 us (level)
    pallas_call x1, Pallas kernels: 42.3 us -> 43.8 us  [local(): pl.pallas_call(gather_kernel, out_shape=(pltpu.VMEM((8192, 1152), bf16),...]
    pallas_call x1, Pallas kernels: 13.9 us -> 12.4 us  [local(): pl.pallas_call(rest_kernel, out_shape=pltpu.VMEM((8192, 1152), bf16), in_...]
where the time goes in v7:
time: 64.2 us; the launch traced here: 64.1 us
  Pallas kernels  63.4 us (99%)
  between operations  0.66 us (1%)
    pallas_call x1, Pallas kernels, local(): pl.pallas_call(gather_kernel, out_shape=(pltpu.VMEM((8192, 1152), bf16),...  43.8 us
    pallas_call x1, Pallas kernels, local(): pl.pallas_call(rest_kernel, out_shape=pltpu.VMEM((8192, 1152), bf16), in_...  12.4 us
    pallas_call x1, Pallas kernels, local(): pl.pallas_call(write_first, out_shape=placed + (jax.ShapeDtypeStruct((1,...  4.52 us
    pallas_call x1, Pallas kernels, local(): pl.pallas_call(write_rest, out_shape=placed, in_specs=[vmem, hbm, hbm, hb...  2.7 us

profile of v7, /device:TPU:1, one launch (start us, length us, event | category | flops | bytes accessed | tf_op | source)
XLA Modules:
  0.0 64.1 jit_solution(6339738276739030267)
XLA Ops:
  0.6 43.8 %gather.1 = (bf16[8192,1152]{1,0:T(8,128)(2,1)S(1)}, f32[1,1152]{1,0:T(1,128)S(1)}) custom-call(f32[256,1024]{1,0:T(8,128)} %one_q.1, f32[256,1024]{1,0:T(8,128)} %other_q.1, f32[64,256]{1,0:T(8,128)} %bitcast.13, f32[64,256]{1,0:T(8,128)} %bitcast.14, f32[64,256]{1,0:T(8,128)} %bitcast.15, f32[64,256]{1,0:T(8,128)} %bitcast.16, f32[1,256]{1,0:T(1,128)} %bitcast.17, ...), custom_call_target="tpu_custom_call" | custom-call | tf_op jit(solution)/shard_map/gather/pallas_call | solution.py:367
  44.4 4.5 %write_first.1 = (bf16[8192,1024]{1,0:T(8,128)(2,1)}, bf16[64,8192]{1,0:T(8,128)(2,1)}, bf16[64,8192]{1,0:T(8,128)(2,1)}, f32[1,1024]{1,0:T(1,128)}, f32[1,64]{1...) custom-call(bf16[8192,1152]{1,0:T(8,128)(2,1)S(1)} %get-tuple-element.18.full.first, ...), custom_call_target="tpu_custom_call" | custom-call | tf_op jit(solution)/shard_map/write_first/pallas_call | solution.py:407
  48.9 12.4 %rest.1.full = bf16[8192,1152]{1,0:T(8,128)(2,1)S(1)} custom-call(bf16[8192,1152]{1,0:T(8,128)(2,1)S(1)} %get-tuple-element.18.full.first, f32[8,128]{1,0:T(8,128)S(1)} %get-tuple-element.20.token), custom_call_target="tpu_custom_call" | custom-call | tf_op jit(solution)/shard_map/rest/pallas_call | solution.py:421
  61.4 2.7 %write_rest.1 = (bf16[8192,1024]{1,0:T(8,128)(2,1)}, bf16[64,8192]{1,0:T(8,128)(2,1)}, bf16[64,8192]{1,0:T(8,128)(2,1)}) custom-call(bf16[8192,1152]{1,0:T(8,128)(2,1)S(1)} %rest.1.full, bf16[8192,1024]{1,0:T(8,128)(2,1)} %get-tuple-element.21.query_in, ...), custom_call_target="tpu_custom_call", output_to_operand_aliasing={{0}: (1, {}), {1}: (2, {}), {2}: (3, {})} | custom-call | tf_op jit(solution)/shard_map/write_rest/pallas_call | solution.py:435
